TPU v7x, 32 devices: a whole 2x2x4 slice. The times are simulated.
32 devices in a mesh: span: 4 (over y, x), model: 8 (over z, core).
Axes of the slice: x: 2, y: 2, z: 4, core: 2. Of those that a mesh axis runs over, the one named last changes fastest.
Arguments:
- latents: bfloat16 [4, 2048, 512], P(None, ('span', 'model')), may hold values from -6 to 6
- rotary_rows: bfloat16 [4, 2048, 64], P(None, ('span', 'model')), may hold values from -6 to 6
- latent_gain: float32 [512], replicated, may hold values from 0.25 to 1.75
- key_up: bfloat16 [512, 16, 128], P(None, 'model'), may hold values from -0.25 to 0.25
- value_up: bfloat16 [512, 16, 128], P(None, 'model'), may hold values from -0.25 to 0.25
Outputs:
- decode_keys: bfloat16 [4, 16, 192, 2048], P('span', 'model')
- decode_values: bfloat16 [4, 2048, 16, 128], P('span', None, 'model')
All inputs are finite; a program needn't handle non-finite values.
Results may differ from a plain program's by a relative error of at most 0.0049.
Values may be sent and summed in bfloat16 or wider, within the bound.
A program may use at most 64 MiB of HBM per device.

v0:
```python
import jax
import jax.numpy as jnp
from jax import lax
from jax.sharding import PartitionSpec as P


def widen_rows(rows, rotary, key_up, value_up):
    wide_keys = jnp.einsum(
        "btr,rhk->bthk", rows, key_up, preferred_element_type=jnp.float32
    ).astype(jnp.bfloat16)
    shared = jnp.broadcast_to(rotary[:, :, None], wide_keys.shape[:3] + rotary.shape[2:])
    wide_values = jnp.einsum(
        "btr,rhk->bthk", rows, value_up, preferred_element_type=jnp.float32
    ).astype(jnp.bfloat16)
    return (jnp.concatenate([wide_keys, shared], axis=-1), wide_values)


def scale_rows(vectors, row_gain):
    return (
        vectors * lax.rsqrt(jnp.mean(vectors * vectors, axis=-1, keepdims=True) + 1e-06) * row_gain
    )


def shards(latents, rotary_rows, latent_gain, key_up, value_up):
    rows_ready = scale_rows(latents.astype(jnp.float32), latent_gain).astype(jnp.bfloat16)
    rows_moved, rotary_moved = (
        lax.all_to_all(rows_ready, "span", split_axis=0, concat_axis=1, tiled=True),
        lax.all_to_all(rotary_rows, "span", split_axis=0, concat_axis=1, tiled=True),
    )
    rows_cut = rows_moved.reshape(
        rows_moved.shape[0], lax.axis_size("span"), -1, rows_moved.shape[2]
    )
    rotary_cut = rotary_moved.reshape(
        rotary_moved.shape[0], lax.axis_size("span"), -1, rotary_moved.shape[2]
    )
    rows_joined, rotary_joined = (
        lax.all_gather(rows_cut, "model", axis=2, tiled=True),
        lax.all_gather(rotary_cut, "model", axis=2, tiled=True),
    )
    rows_whole = rows_joined.reshape(rows_joined.shape[0], -1, rows_joined.shape[3])
    rotary_whole = rotary_joined.reshape(rotary_joined.shape[0], -1, rotary_joined.shape[3])
    decode_keys, decode_values = widen_rows(rows_whole, rotary_whole, key_up, value_up)
    decode_keys = jnp.transpose(decode_keys, (0, 2, 3, 1))
    return (decode_keys, decode_values)


def solution(mesh):
    placed = (
        P(None, ("span", "model"), None),
        P(None, ("span", "model"), None),
        P(),
        P(None, "model", None),
        P(None, "model", None),
    )
    return jax.shard_map(
        shards,
        mesh=mesh,
        in_specs=placed,
        out_specs=(P("span", "model", None, None), P("span", None, "model", None)),
        check_vma=False,
    )
```

profile of v0, /device:TPU:1, one launch (start us, length us, event | category | flops | bytes accessed | tf_op | source)
XLA Modules:
  0.0 75.5 jit_solution(13271837886487071858)
XLA Ops:
  7.2 0.0 copy-start
  7.2 0.0 all-gather.4.cloned.1.call-start
  7.2 1.1 %fusion.1 = f32[4,64]{1,0:T(4,128)S(1)} fusion(bf16[4,64,512]{2,1,0:T(8,128)(2,1)} %param.5), kind=kLoop, calls=%fused_computation.6 | loop fusion | flops 392960 | bytes 263168 | tf_op jit(solution)/shard_map/reduce_sum | solution.py:20
  8.4 1.1 %fusion.3 = bf16[4,64,512]{2,1,0:T(8,128)(2,1)S(1)} fusion(bf16[4,64,512]{2,1,0:T(8,128)(2,1)} %param.5, f32[512]{0:T(512)} %param.7, f32[4,64]{1,0:T(4,128)S(1)} %add_rsqrt_fusion), kind=kLoop, calls=%fused_computation.8 | loop fusion | flops 524288 | bytes 527360 | tf_op jit(solution)/shard_map/convert_element_type | solution.py:25
  9.4 8.8 %all_to_all.8 = bf16[4,64,512]{2,1,0:T(8,128)(2,1)} all-to-all(bf16[4,64,512]{2,1,0:T(8,128)(2,1)S(1)} %fusion.3), channel_id=1, replica_groups=mesh['span'=4,'model'=8] {'span'}, dimensions={0} | all-to-all | bytes 524288 | tf_op jit(solution)/shard_map/all_to_all | solution.py:27
  18.3 0.0 all-gather.4.cloned.1.call-update
  18.3 1.6 %reshape.51 = bf16[4,2,2048]{2,1,0:T(2,128)(2,1)} reshape(bf16[4,64,64]{2,1,0:T(8,128)(2,1)} %param.6) | data formatting | bytes 65536
  19.9 3.3 %all-to-all-start.1 = ((bf16[4,2,2048]{2,1,0:T(2,128)(2,1)}), bf16[4,2,2048]{2,1,0:T(2,128)(2,1)S(1)}, u32[]{:S(2)}, u32[]{:S(2)}) async-start(bf16[4,2,2048]{2,1,0:T(2,128)(2,1)} %reshape.51), calls=%async_computation.1 | async-start | bytes 65536 | tf_op jit(solution)/shard_map/all_to_all | solution.py:28
  23.1 1.1 %copy.7 = bf16[512,2,128]{0,2,1:T(8,128)(2,1)S(1)} copy(bf16[512,2,128]{2,1,0:T(2,128)(2,1)} %param.8) | data formatting | bytes 524288 | tf_op args[3]
  24.3 2.5 %all-to-all-done.1 = bf16[4,2,2048]{2,1,0:T(2,128)(2,1)S(1)} async-done(((bf16[4,2,2048]{2,1,0:T(2,128)(2,1)}), bf16[4,2,2048]{2,1,0:T(2,128)(2,1)S(1)}, u32[]{:S(2)}, u32[]{:S(2)}) %all-to-all-start.1) | async-done | bytes 32800 | tf_op jit(solution)/shard_map/all_to_all | solution.py:28
  26.7 0.1 reshape.52
  26.8 20.8 %all-gather.1 = bf16[4,512,64]{2,1,0:T(8,128)(2,1)S(1)} all-gather(bf16[4,64,64]{2,1,0:T(8,128)(2,1)S(1)} %reshape.52), channel_id=3, replica_groups=mesh['span'=4,'model'=8] {'model'}, dimensions={1}, use_global_device_ids=true | all-gather | bytes 294912 | tf_op jit(solution)/shard_map/all_gather | solution.py:38
  47.6 0.2 copy.8
  47.9 5.4 %all-gather.4.cloned.1.call-done = bf16[4,512,512]{2,1,0:T(8,128)(2,1)} async-done(((bf16[4,64,512]{2,1,0:T(8,128)(2,1)}), bf16[4,512,512]{2,1,0:T(8,128)(2,1)}) %all-gather.4.cloned.1.call-update) | async-done | bytes 2097168 | tf_op jit(solution)/shard_map/all_gather | solution.py:37
  53.3 2.3 %fusion.5 = f32[2048,256]{0,1:S(1)} fusion(bf16[2048,512]{1,0:T(8,128)(2,1)} %bitcast.16, bf16[512,256]{0,1:T(8,128)(2,1)S(1)} %bitcast.19), kind=kOutput, calls=%fused_computation.11 | convolution fusion | flops 536870912 | bytes 4456448
  55.6 0.0 copy-start.1
  55.6 0.1 convert_bitcast_fusion
  55.8 0.0 copy-done
  55.8 1.4 %copy-done.1 = bf16[4,512,512]{2,1,0:T(8,128)(2,1)S(1)} copy-done((bf16[4,512,512]{2,1,0:T(8,128)(2,1)S(1)}, bf16[4,512,512]{2,1,0:T(8,128)(2,1)}, u32[]{:S(2)}) %copy-start.1) | copy-done | bytes 2097176
  57.2 0.7 fusion
  57.9 9.5 %copy.10 = bf16[1,2048,2,128]{3,2,1,0:T(2,128)(2,1)} copy(bf16[1,2048,2,128]{3,1,2,0:T(8,128)(2,1)S(1)} %fusion) | data formatting | bytes 2097152
  67.4 1.2 %maximum_bitcast_fusion = bf16[1,2,192,2048]{3,2,1,0:T(8,128)(2,1)} fusion(bf16[1,2048,2,64]{1,3,2,0:T(8,128)(2,1)S(1)} %broadcast_in_dim.10, bf16[1,2048,2,128]{1,3,2,0:T(8,128)(2,1)S(1)} %convert_bitcast_fusion), kind=kLoop, calls=%fused_computation.2 | loop fusion | flops 3145728 | bytes 3145728 | tf_op jit(solution)/shard_map/transpose | solution.py:43
  (2 shorter events, 0.0 us)
Async XLA Ops:
  7.2 48.6 %copy-start = (bf16[512,2,128]{2,1,0:T(2,128)(2,1)S(1)}, bf16[512,2,128]{2,1,0:T(2,128)(2,1)}, u32[]{:S(2)}) copy-start(bf16[512,2,128]{2,1,0:T(2,128)(2,1)} %param.9) | copy-start | bytes 786436
  7.2 46.1 %all-gather.4.cloned.1.call-start = ((), (), s32[]{:S(2)}) async-start(), calls=%async_computation.2 | async-start | bytes 2359296 | tf_op jit(solution)/shard_map/all_gather | solution.py:37
  19.9 6.8 %all-to-all-start.1 = ((bf16[4,2,2048]{2,1,0:T(2,128)(2,1)}), bf16[4,2,2048]{2,1,0:T(2,128)(2,1)S(1)}, u32[]{:S(2)}, u32[]{:S(2)}) async-start(bf16[4,2,2048]{2,1,0:T(2,128)(2,1)} %reshape.51), calls=%async_computation.1 | async-start | bytes 65536 | tf_op jit(solution)/shard_map/all_to_all | solution.py:28
  55.6 1.6 %copy-start.1 = (bf16[4,512,512]{2,1,0:T(8,128)(2,1)S(1)}, bf16[4,512,512]{2,1,0:T(8,128)(2,1)}, u32[]{:S(2)}) copy-start(bf16[4,512,512]{2,1,0:T(8,128)(2,1)} %all-gather.4.cloned.1.call-done) | copy-start | bytes 6291460
Sparse Core Ops, SparseCore 0:
  18.4 34.7 all-gather.3
where the time goes:
time: 76.2 us; the launch traced here: 75.5 us
  blocking collectives  29.6 us (39%)
  between operations  14.1 us (19%)
  local copies, waits for them, and re-layouts  13.9 us (18%)
  waiting for transfers between devices  7.88 us (10%)
  other arithmetic  3.59 us (5%)
  starting transfers between devices  3.3 us (4%)
  matrix products  3.03 us (4%)
    all_gather x1, blocking collectives, shards(): lax.all_gather(rotary_cut, 'model', axis=2, tiled=True)  20.8 us
    unnamed x8, local copies, waits for them, and re-layouts  13.7 us
    all_to_all x1, blocking collectives, shards(): lax.all_to_all(rows_ready, 'span', split_axis=0, concat_axis=1, tiled=True)  8.83 us
    all_gather x1, waiting for transfers between devices, shards(): lax.all_gather(rows_cut, 'model', axis=2, tiled=True)  5.41 us
    all_to_all x1, starting transfers between devices, shards(): lax.all_to_all(rotary_rows, 'span', split_axis=0, concat_axis=1, tiled=True)  3.26 us
    all_to_all x1, waiting for transfers between devices, shards(): lax.all_to_all(rotary_rows, 'span', split_axis=0, concat_axis=1, tiled=True)  2.45 us
    unnamed x1, matrix products  2.33 us
  transfers between devices with their start and end apart: 2, of which 2 were waited for; matrix products, arithmetic and copies ran while one was open for 4% of the time, Pallas kernels for 0%

commit v1 on v0

v1 whole, which is shorter than its diff:
```python
import functools

import jax
import jax.numpy as jnp
from jax import lax
from jax.experimental import pallas as pl
from jax.experimental.pallas import tpu as pltpu
from jax.sharding import PartitionSpec as P

CORES = 2
LANES = 128


def gather_expand(
    spans,
    levels,
    latents,
    rotary,
    gain_ref,
    key_up,
    value_up,
    keys_out,
    values_out,
    mine,
    rotary_raw,
    rotary_mine,
    rows,
    turned,
    wide,
    key_weights,
    value_weights,
    mixed,
    local_sem,
    cross_sem,
    up_sem,
    down_sem,
    pair_sem,
    got_sem,
    pair_got_sem,
):
    span = lax.axis_index("span")
    model = lax.axis_index("model")
    level, core = model // CORES, model % CORES
    length, latent = latents.shape[1], latents.shape[2]
    rotary_size = rotary.shape[2]
    half = length // 2
    heads, key_size = keys_out.shape[0], wide.shape[1]
    has_up, has_down = level < levels - 1, level > 0

    def device(to_span, to_level, to_core):
        return {"span": to_span, "model": to_level * CORES + to_core}

    above = device(span, level + 1, core)
    below = device(span, level - 1, core)
    pair = device(span, level, 1 - core)

    def first_row(origin, plane):
        return (origin * levels + plane) * (CORES * length)

    def place(part, origin, plane, of_core):
        start = first_row(origin, plane) + of_core * length
        if part == 0:
            return rows.at[pl.ds(pl.multiple_of(start, length), length)]
        return turned.at[pl.ds(pl.multiple_of(start // 2, half), half)]

    def send(part, origin, plane, source, target, send_sem, recv_sem):
        slot = origin * levels + plane
        here = place(part, origin, plane, core)
        return pltpu.make_async_remote_copy(
            src_ref=here if source is None else source,
            dst_ref=here,
            send_sem=send_sem.at[slot, part],
            recv_sem=recv_sem.at[slot, part],
            device_id=target,
            device_id_type=pl.DeviceIdType.MESH,
        )

    def cross(part, step):
        to_span = lax.rem(span + (spans - step), spans)
        source = mine if part == 0 else rotary_mine
        return pltpu.make_async_remote_copy(
            src_ref=source.at[to_span],
            dst_ref=place(part, span, level, core),
            send_sem=cross_sem.at[step, part],
            recv_sem=got_sem.at[span * levels + level, part],
            device_id=device(to_span, level, core),
            device_id_type=pl.DeviceIdType.MESH,
        )

    def arrived(part, origin, plane):
        send(part, origin, plane, None, pair, pair_sem, got_sem).wait_recv()

    def pair_arrived(origin, plane):
        for part in range(2):
            slot = origin * levels + plane
            there = place(part, origin, plane, 1 - core)
            pltpu.make_async_remote_copy(
                src_ref=there,
                dst_ref=there,
                send_sem=pair_sem.at[slot, part],
                recv_sem=pair_got_sem.at[slot, part],
                device_id=pair,
                device_id_type=pl.DeviceIdType.MESH,
            ).wait_recv()

    barrier = pltpu.get_barrier_semaphore()

    def greet(target):
        pl.semaphore_signal(
            barrier, inc=1, device_id=target, device_id_type=pl.DeviceIdType.MESH
        )

    @pl.when(has_up)
    def _():
        greet(above)

    @pl.when(has_down)
    def _():
        greet(below)

    greet(pair)
    for step in range(1, spans):
        greet(device(lax.rem(span + step, spans), level, core))

    local = [
        pltpu.make_async_copy(latents, mine, local_sem.at[0]),
        pltpu.make_async_copy(rotary, rotary_raw, local_sem.at[1]),
        pltpu.make_async_copy(
            latents.at[span], place(0, span, level, core), local_sem.at[2]
        ),
    ]
    for copy in local:
        copy.start()
    local[1].wait()
    for sequence in range(spans):
        rotary_mine[sequence] = jnp.concatenate(
            [rotary_raw[sequence, :half], rotary_raw[sequence, half:]], axis=1
        )
    place(1, span, level, core)[...] = rotary_mine[span]
    local[0].wait()
    pl.semaphore_wait(
        barrier, spans + has_up.astype(jnp.int32) + has_down.astype(jnp.int32)
    )

    own = (mine.at[span], rotary_mine.at[span])
    for part in range(2):

        @pl.when(has_up)
        def _():
            send(part, span, level, own[part], above, up_sem, got_sem).start()

        @pl.when(has_down)
        def _():
            send(part, span, level, own[part], below, down_sem, got_sem).start()

        for step in range(1, spans):
            cross(part, step).start()
        send(part, span, level, own[part], pair, pair_sem, pair_got_sem).start()

    wide[...] = key_up[...].astype(jnp.float32)
    for head in range(heads):
        weight = wide[pl.ds(head, latent, stride=heads), :] if heads > 1 else wide[...]
        key_weights[head * key_size : (head + 1) * key_size, :] = weight.T.astype(
            jnp.bfloat16
        )
    wide[...] = value_up[...].astype(jnp.float32)
    for head in range(heads):
        weight = wide[pl.ds(head, latent, stride=heads), :] if heads > 1 else wide[...]
        value_weights[:, head * key_size : (head + 1) * key_size] = weight.astype(
            jnp.bfloat16
        )
    local[2].wait()

    def expand(start, count):
        block = rows[pl.ds(pl.multiple_of(start, count), count), :].astype(jnp.float32)
        scale = lax.rsqrt(jnp.mean(block * block, axis=-1, keepdims=True) + 1e-06)
        ready = (block * scale * gain_ref[...]).astype(jnp.bfloat16)
        lanes = pl.ds(pl.multiple_of(start, count), count)
        keys = lax.dot_general(
            key_weights[...],
            ready,
            (((1,), (1,)), ((), ())),
            preferred_element_type=jnp.float32,
        ).astype(jnp.bfloat16)
        packed = turned[
            pl.ds(pl.multiple_of(start // 2, count // 2), count // 2), :
        ].astype(jnp.float32)
        pieces = []
        for first in range(0, count // 2, half):
            piece = packed[first : first + half]
            pieces += [piece, pltpu.roll(piece, rotary_size, 1)]
        shared = jnp.concatenate(pieces, axis=0).T[:rotary_size].astype(jnp.bfloat16)
        for head in range(heads):
            keys_out[head, :key_size, lanes] = keys[
                head * key_size : (head + 1) * key_size
            ]
            keys_out[head, key_size:, lanes] = shared
        values = jnp.dot(
            ready, value_weights[...], preferred_element_type=jnp.float32
        )
        if heads > 1:
            for head in range(heads):
                mixed[pl.ds(head, count, stride=heads), :] = values[
                    :, head * key_size : (head + 1) * key_size
                ]
            values = mixed[...]
        values_out[
            pl.ds(pl.multiple_of(start * heads, count * heads), count * heads), :
        ] = values.astype(jnp.bfloat16)

    chunk = mixed.shape[0] // heads
    early = chunk == CORES * length

    def finish(origin, plane):
        pair_arrived(origin, plane)
        if early:
            expand(first_row(origin, plane), chunk)

    def origin_of(step):
        return lax.rem(span + step, spans)

    def own_level(step, _):
        origin = origin_of(step)
        for part in range(2):
            arrived(part, origin, level)

            @pl.when(has_up)
            def _():
                send(part, origin, level, None, above, up_sem, got_sem).start()

            @pl.when(has_down)
            def _():
                send(part, origin, level, None, below, down_sem, got_sem).start()

            send(part, origin, level, None, pair, pair_sem, pair_got_sem).start()
        finish(origin_of(step - 1), level)
        return 0

    lax.fori_loop(1, spans, own_level, 0)

    def pass_on(step, _):
        away = 1 + step // spans
        origin = origin_of(lax.rem(step, spans))
        for plane, exists, more, target, sem in (
            (level - away, level >= away, has_up, above, up_sem),
            (level + away, level + away < levels, has_down, below, down_sem),
        ):

            @pl.when(exists)
            def _():
                for part in range(2):
                    arrived(part, origin, plane)

                    @pl.when(more)
                    def _():
                        send(part, origin, plane, None, target, sem, got_sem).start()

                    send(part, origin, plane, None, pair, pair_sem, pair_got_sem).start()

        finish_step(step - 1)
        return 0

    def finish_step(step):
        @pl.when(step < 0)
        def _():
            finish(origin_of(spans - 1), level)

        away = 1 + step // spans
        origin = origin_of(lax.rem(step + spans, spans))

        @pl.when((step >= 0) & (level >= away))
        def _():
            finish(origin, level - away)

        @pl.when((step >= 0) & (level + away < levels))
        def _():
            finish(origin, level + away)

    steps = (levels - 1) * spans
    lax.fori_loop(0, steps, pass_on, 0)
    finish_step(steps - 1)

    if not early:

        def late(step, _):
            expand(step * chunk, chunk)
            return 0

        lax.fori_loop(0, rows.shape[0] // chunk, late, 0)

    def drain(slot, _):
        origin, plane = slot // levels, slot % levels
        for part in range(2):

            @pl.when(has_up & (plane <= level))
            def _():
                send(part, origin, plane, None, above, up_sem, got_sem).wait_send()

            @pl.when(has_down & (plane >= level))
            def _():
                send(part, origin, plane, None, below, down_sem, got_sem).wait_send()

            send(part, origin, plane, None, pair, pair_sem, pair_got_sem).wait_send()
        return 0

    lax.fori_loop(0, spans * levels, drain, 0)
    for step in range(1, spans):
        for part in range(2):
            cross(part, step).wait_send()


def shards(spans, levels, latents, rotary_rows, latent_gain, key_up, value_up):
    sequences, length, latent = latents.shape
    rotary_size = rotary_rows.shape[2]
    heads, key_size = key_up.shape[1:]
    total = spans * levels * CORES * length
    chunk = max(CORES * length, LANES)
    vmem = pl.BlockSpec(memory_space=pltpu.VMEM)
    hbm = pl.BlockSpec(memory_space=pl.ANY)
    slots = spans * levels
    sems = pltpu.SemaphoreType.DMA
    keys, values = pl.pallas_call(
        functools.partial(gather_expand, spans, levels),
        out_shape=(
            jax.ShapeDtypeStruct((heads, key_size + rotary_size, total), jnp.bfloat16),
            jax.ShapeDtypeStruct((total * heads, key_size), jnp.bfloat16),
        ),
        in_specs=[hbm, hbm, vmem, vmem, vmem],
        out_specs=(vmem, vmem),
        scratch_shapes=[
            pltpu.VMEM(latents.shape, jnp.bfloat16),
            pltpu.VMEM(rotary_rows.shape, jnp.bfloat16),
            pltpu.VMEM((sequences, length // 2, 2 * rotary_size), jnp.bfloat16),
            pltpu.VMEM((total, latent), jnp.bfloat16),
            pltpu.VMEM((total // 2, 2 * rotary_size), jnp.bfloat16),
            pltpu.VMEM((latent * heads, key_size), jnp.float32),
            pltpu.VMEM((heads * key_size, latent), jnp.bfloat16),
            pltpu.VMEM((latent, heads * key_size), jnp.bfloat16),
            pltpu.VMEM((chunk * heads, key_size), jnp.float32),
            sems((3,)),
            sems((spans, 2)),
            sems((slots, 2)),
            sems((slots, 2)),
            sems((slots, 2)),
            sems((slots, 2)),
            sems((slots, 2)),
        ],
        compiler_params=pltpu.CompilerParams(
            collective_id=0, has_side_effects=True, vmem_limit_bytes=40 * 1024 * 1024
        ),
    )(
        latents,
        rotary_rows,
        latent_gain.reshape(1, latent),
        key_up.reshape(latent * heads, key_size),
        value_up.reshape(latent * heads, key_size),
    )
    return keys[None], values.reshape(1, total, heads, key_size)


def solution(mesh):
    placed = (
        P(None, ("span", "model"), None),
        P(None, ("span", "model"), None),
        P(),
        P(None, "model", None),
        P(None, "model", None),
    )
    spans, levels = mesh.shape["span"], mesh.shape["model"] // CORES
    return jax.shard_map(
        functools.partial(shards, spans, levels),
        mesh=mesh,
        in_specs=placed,
        out_specs=(P("span", "model", None, None), P("span", None, "model", None)),
        check_vma=False,
    )
```

time: 76.2 us -> 36.9 us (0.48)
  blocking collectives: 29.6 us -> 0 us
  Pallas kernels: 0 us -> 29.5 us
  between operations: 14.1 us -> 0.65 us
  waiting for transfers between devices: 7.88 us -> 0 us
  local copies, waits for them, and re-layouts: 13.9 us -> 6.48 us
  other arithmetic: 3.59 us -> 0 us
  starting transfers between devices: 3.3 us -> 0 us
  matrix products: 3.03 us -> 0 us
    pallas_call x0 -> x1, Pallas kernels: none -> 29.5 us  [shards(): pl.pallas_call(functools.partial(gather_expand, spans, levels), out_shape...]
    all_gather x1 -> x0, blocking collectives: 20.8 us -> none  [shards(): lax.all_gather(rotary_cut, 'model', axis=2, tiled=True)]
    all_to_all x1 -> x0, blocking collectives: 8.83 us -> none  [shards(): lax.all_to_all(rows_ready, 'span', split_axis=0, concat_axis=1, tiled=True)]
    unnamed x8 -> x12, local copies, waits for them, and re-layouts: 13.7 us -> 6.48 us
    all_gather x1 -> x0, waiting for transfers between devices: 5.41 us -> none  [shards(): lax.all_gather(rows_cut, 'model', axis=2, tiled=True)]
    all_to_all x1 -> x0, starting transfers between devices: 3.26 us -> none  [shards(): lax.all_to_all(rotary_rows, 'span', split_axis=0, concat_axis=1, tiled=True)]
    all_to_all x1 -> x0, waiting for transfers between devices: 2.45 us -> none  [shards(): lax.all_to_all(rotary_rows, 'span', split_axis=0, concat_axis=1, tiled=True)]
    unnamed x1 -> x0, matrix products: 2.33 us -> none
  transfers between devices with their start and end apart: 2 -> 0, of which waited for: 2 -> 0; matrix products, arithmetic and copies ran while one was open for 4% -> 0% of each run, Pallas kernels for 0% -> 0%
where the time goes in v1:
time: 36.9 us; the launch traced here: 36.6 us
  Pallas kernels  29.5 us (80%)
  local copies, waits for them, and re-layouts  6.48 us (18%)
  between operations  0.65 us (2%)
    pallas_call x1, Pallas kernels, shards(): pl.pallas_call(functools.partial(gather_expand, spans, levels), out_shape...  29.5 us
    unnamed x12, local copies, waits for them, and re-layouts  6.48 us

profile of v1, /device:TPU:1, one launch (start us, length us, event | category | flops | bytes accessed | tf_op | source)
XLA Modules:
  0.0 36.6 jit_solution(2110376606788184103)
XLA Ops:
  0.6 0.0 copy-start
  0.6 0.9 %copy-done = bf16[4,64,512]{2,1,0:T(8,128)(2,1)S(1)} copy-done((bf16[4,64,512]{2,1,0:T(8,128)(2,1)S(1)}, bf16[4,64,512]{2,1,0:T(8,128)(2,1)}, u32[]{:S(2)}) %copy-start) | copy-done | bytes 262168
  1.6 0.0 copy-start.1
  1.6 0.9 %copy-done.1 = bf16[512,2,128]{2,1,0:T(2,128)(2,1)S(1)} copy-done((bf16[512,2,128]{2,1,0:T(2,128)(2,1)S(1)}, bf16[512,2,128]{2,1,0:T(2,128)(2,1)}, u32[]{:S(2)}) %copy-start.1) | copy-done | bytes 262168
  2.5 0.0 copy-start.2
  2.5 0.9 %copy-done.2 = bf16[512,2,128]{2,1,0:T(2,128)(2,1)S(1)} copy-done((bf16[512,2,128]{2,1,0:T(2,128)(2,1)S(1)}, bf16[512,2,128]{2,1,0:T(2,128)(2,1)}, u32[]{:S(2)}) %copy-start.2) | copy-done | bytes 262168
  3.5 0.0 copy-start.3
  3.5 0.8 %copy-done.3 = bf16[4,64,64]{2,1,0:T(8,128)(2,1)S(1)} copy-done((bf16[4,64,64]{2,1,0:T(8,128)(2,1)S(1)}, bf16[4,64,64]{2,1,0:T(8,128)(2,1)}, u32[]{:S(2)}) %copy-start.3) | copy-done | bytes 32792
  4.3 0.0 copy-start.4
  4.3 0.7 %copy-done.4 = f32[512]{0:T(512)S(1)} copy-done((f32[512]{0:T(512)S(1)}, f32[512]{0:T(512)}, u32[]{:S(2)}) %copy-start.4) | copy-done | bytes 2072
  5.0 29.5 %shard_map.68 = (bf16[2,192,2048]{2,1,0:T(8,128)(2,1)S(1)}, bf16[4096,128]{1,0:T(8,128)(2,1)S(1)}) custom-call(bf16[4,64,512]{2,1,0:T(8,128)(2,1)S(1)} %copy-done, bf16[4,64,64]{2,1,0:T(8,128)(2,1)S(1)} %copy-done.3, f32[1,512]{1,0:T(1,128)S(1)} %bitcast.9, bf16[1024,128]{1,0:T(8,128)(2,1)S(1)} %bitcast.7, bf16[1024,128]{1,0:T(8,128)(2,1)S(1)} %bitcast.8), custom_call_target="tpu_custom_call" | custom-call | tf_op jit(solution)/shard_map/pallas_call | solution.py:322
  34.5 1.1 %copy.9 = bf16[1,2,192,2048]{3,2,1,0:T(8,128)(2,1)} copy(bf16[1,2,192,2048]{3,2,1,0:T(8,128)(2,1)S(1)} %bitcast.5) | data formatting | bytes 3145728
  35.6 1.0 %copy.10 = bf16[1,2048,2,128]{3,2,1,0:T(2,128)(2,1)} copy(bf16[1,2048,2,128]{3,2,1,0:T(2,128)(2,1)S(1)} %bitcast.6) | data formatting | bytes 2097152
Async XLA Ops:
  0.6 1.0 %copy-start = (bf16[4,64,512]{2,1,0:T(8,128)(2,1)S(1)}, bf16[4,64,512]{2,1,0:T(8,128)(2,1)}, u32[]{:S(2)}) copy-start(bf16[4,64,512]{2,1,0:T(8,128)(2,1)} %latents.1) | copy-start | bytes 786436
  1.6 0.9 %copy-start.1 = (bf16[512,2,128]{2,1,0:T(2,128)(2,1)S(1)}, bf16[512,2,128]{2,1,0:T(2,128)(2,1)}, u32[]{:S(2)}) copy-start(bf16[512,2,128]{2,1,0:T(2,128)(2,1)} %param.8) | copy-start | bytes 786436
  2.5 0.9 %copy-start.2 = (bf16[512,2,128]{2,1,0:T(2,128)(2,1)S(1)}, bf16[512,2,128]{2,1,0:T(2,128)(2,1)}, u32[]{:S(2)}) copy-start(bf16[512,2,128]{2,1,0:T(2,128)(2,1)} %param.9) | copy-start | bytes 786436
  3.5 0.8 %copy-start.3 = (bf16[4,64,64]{2,1,0:T(8,128)(2,1)S(1)}, bf16[4,64,64]{2,1,0:T(8,128)(2,1)}, u32[]{:S(2)}) copy-start(bf16[4,64,64]{2,1,0:T(8,128)(2,1)} %rotary.1) | copy-start | bytes 98308
  4.3 0.7 %copy-start.4 = (f32[512]{0:T(512)S(1)}, f32[512]{0:T(512)}, u32[]{:S(2)}) copy-start(f32[512]{0:T(512)} %param.7) | copy-start | bytes 6148

commit v2 on v1

--- a/solution.py
+++ b/solution.py
@@ -9,6 +9,7 @@
 
 CORES = 2
 LANES = 128
+VMEM_BYTES = 67043328
 
 
 def gather_expand(
@@ -16,7 +17,7 @@
     levels,
     latents,
     rotary,
-    gain_ref,
+    gain,
     key_up,
     value_up,
     keys_out,
@@ -26,6 +27,9 @@
     rotary_mine,
     rows,
     turned,
+    gain_ref,
+    key_raw,
+    value_raw,
     wide,
     key_weights,
     value_weights,
@@ -75,15 +79,15 @@
             device_id_type=pl.DeviceIdType.MESH,
         )
 
-    def cross(part, step):
+    def cross(part, step, towards):
         to_span = lax.rem(span + (spans - step), spans)
         source = mine if part == 0 else rotary_mine
         return pltpu.make_async_remote_copy(
             src_ref=source.at[to_span],
             dst_ref=place(part, span, level, core),
-            send_sem=cross_sem.at[step, part],
+            send_sem=cross_sem.at[towards + 1, step, part],
             recv_sem=got_sem.at[span * levels + level, part],
-            device_id=device(to_span, level, core),
+            device_id=device(to_span, level + towards, core),
             device_id_type=pl.DeviceIdType.MESH,
         )
 
@@ -110,66 +114,99 @@
             barrier, inc=1, device_id=target, device_id_type=pl.DeviceIdType.MESH
         )
 
-    @pl.when(has_up)
-    def _():
-        greet(above)
-
-    @pl.when(has_down)
-    def _():
-        greet(below)
-
+    for step in range(spans):
+        to_span = lax.rem(span + step, spans)
+
+        @pl.when(has_up)
+        def _():
+            greet(device(to_span, level + 1, core))
+
+        @pl.when(has_down)
+        def _():
+            greet(device(to_span, level - 1, core))
+
+        if step > 0:
+            greet(device(to_span, level, core))
     greet(pair)
-    for step in range(1, spans):
-        greet(device(lax.rem(span + step, spans), level, core))
 
     local = [
-        pltpu.make_async_copy(latents, mine, local_sem.at[0]),
-        pltpu.make_async_copy(rotary, rotary_raw, local_sem.at[1]),
-        pltpu.make_async_copy(
-            latents.at[span], place(0, span, level, core), local_sem.at[2]
-        ),
+        pltpu.make_async_copy(source, target, local_sem.at[index])
+        for index, (source, target) in enumerate(
+            (
+                (rotary, rotary_raw),
+                (latents, mine),
+                (latents.at[span], place(0, span, level, core)),
+                (key_up, key_raw),
+                (value_up, value_raw),
+                (gain, gain_ref),
+            )
+        )
     ]
     for copy in local:
         copy.start()
-    local[1].wait()
+    local[0].wait()
     for sequence in range(spans):
         rotary_mine[sequence] = jnp.concatenate(
             [rotary_raw[sequence, :half], rotary_raw[sequence, half:]], axis=1
         )
     place(1, span, level, core)[...] = rotary_mine[span]
-    local[0].wait()
+    local[1].wait()
     pl.semaphore_wait(
-        barrier, spans + has_up.astype(jnp.int32) + has_down.astype(jnp.int32)
+        barrier,
+        spans
+        + spans * has_up.astype(jnp.int32)
+        + spans * has_down.astype(jnp.int32),
     )
 
-    own = (mine.at[span], rotary_mine.at[span])
-    for part in range(2):
-
-        @pl.when(has_up)
-        def _():
-            send(part, span, level, own[part], above, up_sem, got_sem).start()
-
-        @pl.when(has_down)
-        def _():
-            send(part, span, level, own[part], below, down_sem, got_sem).start()
-
-        for step in range(1, spans):
-            cross(part, step).start()
-        send(part, span, level, own[part], pair, pair_sem, pair_got_sem).start()
-
-    wide[...] = key_up[...].astype(jnp.float32)
+    upper = level * 2 >= levels
+
+    def start_towards(towards, steps):
+        for step in steps:
+            for part in range(2):
+                cross(part, step, towards).start()
+
+    def start_adjacent(steps):
+        @pl.when(upper)
+        def _():
+            @pl.when(has_up)
+            def _():
+                start_towards(1, steps)
+
+            start_towards(-1, steps)
+
+        @pl.when(jnp.logical_not(upper))
+        def _():
+            @pl.when(has_down)
+            def _():
+                start_towards(-1, steps)
+
+            start_towards(1, steps)
+
+    if levels > 1:
+        start_adjacent(range(1))
+        start_adjacent(range(1, spans))
+    start_towards(0, range(1, spans))
+    for part, own in enumerate((mine, rotary_mine)):
+        send(
+            part, span, level, own.at[span], pair, pair_sem, pair_got_sem
+        ).start()
+
+    local[3].wait()
+    wide[...] = key_raw[...].astype(jnp.float32)
     for head in range(heads):
         weight = wide[pl.ds(head, latent, stride=heads), :] if heads > 1 else wide[...]
         key_weights[head * key_size : (head + 1) * key_size, :] = weight.T.astype(
             jnp.bfloat16
         )
-    wide[...] = value_up[...].astype(jnp.float32)
+    local[4].wait()
+    wide[...] = value_raw[...].astype(jnp.float32)
     for head in range(heads):
         weight = wide[pl.ds(head, latent, stride=heads), :] if heads > 1 else wide[...]
         value_weights[:, head * key_size : (head + 1) * key_size] = weight.astype(
             jnp.bfloat16
         )
     local[2].wait()
+    local[5].wait()
 
     def expand(start, count):
         block = rows[pl.ds(pl.multiple_of(start, count), count), :].astype(jnp.float32)
@@ -219,24 +256,8 @@
     def origin_of(step):
         return lax.rem(span + step, spans)
 
-    def own_level(step, _):
-        origin = origin_of(step)
-        for part in range(2):
-            arrived(part, origin, level)
-
-            @pl.when(has_up)
-            def _():
-                send(part, origin, level, None, above, up_sem, got_sem).start()
-
-            @pl.when(has_down)
-            def _():
-                send(part, origin, level, None, below, down_sem, got_sem).start()
-
-            send(part, origin, level, None, pair, pair_sem, pair_got_sem).start()
-        finish(origin_of(step - 1), level)
-        return 0
-
-    lax.fori_loop(1, spans, own_level, 0)
+    def own_turn(step):
+        return (step >= spans) & (step < 2 * spans)
 
     def pass_on(step, _):
         away = 1 + step // spans
@@ -255,28 +276,35 @@
                     def _():
                         send(part, origin, plane, None, target, sem, got_sem).start()
 
+                for part in range(2):
                     send(part, origin, plane, None, pair, pair_sem, pair_got_sem).start()
 
-        finish_step(step - 1)
+        @pl.when(own_turn(step) & (step > spans))
+        def _():
+            for part in range(2):
+                arrived(part, origin, level)
+                send(part, origin, level, None, pair, pair_sem, pair_got_sem).start()
+
+        @pl.when(step > 0)
+        def _():
+            finish_step(step - 1)
+
         return 0
 
     def finish_step(step):
-        @pl.when(step < 0)
-        def _():
-            finish(origin_of(spans - 1), level)
-
         away = 1 + step // spans
-        origin = origin_of(lax.rem(step + spans, spans))
-
-        @pl.when((step >= 0) & (level >= away))
-        def _():
-            finish(origin, level - away)
-
-        @pl.when((step >= 0) & (level + away < levels))
-        def _():
-            finish(origin, level + away)
-
-    steps = (levels - 1) * spans
+        origin = origin_of(lax.rem(step, spans))
+        for plane, exists in (
+            (level - away, level >= away),
+            (level + away, level + away < levels),
+            (level, own_turn(step)),
+        ):
+
+            @pl.when(exists)
+            def _():
+                finish(origin, plane)
+
+    steps = max(levels - 1, 2) * spans
     lax.fori_loop(0, steps, pass_on, 0)
     finish_step(steps - 1)
 
@@ -292,11 +320,11 @@
         origin, plane = slot // levels, slot % levels
         for part in range(2):
 
-            @pl.when(has_up & (plane <= level))
+            @pl.when(has_up & (plane < level))
             def _():
                 send(part, origin, plane, None, above, up_sem, got_sem).wait_send()
 
-            @pl.when(has_down & (plane >= level))
+            @pl.when(has_down & (plane > level))
             def _():
                 send(part, origin, plane, None, below, down_sem, got_sem).wait_send()
 
@@ -304,9 +332,19 @@
         return 0
 
     lax.fori_loop(0, spans * levels, drain, 0)
-    for step in range(1, spans):
+    for step in range(spans):
         for part in range(2):
-            cross(part, step).wait_send()
+
+            @pl.when(has_up)
+            def _():
+                cross(part, step, 1).wait_send()
+
+            @pl.when(has_down)
+            def _():
+                cross(part, step, -1).wait_send()
+
+            if step > 0:
+                cross(part, step, 0).wait_send()
 
 
 def shards(spans, levels, latents, rotary_rows, latent_gain, key_up, value_up):
@@ -316,8 +354,9 @@
     total = spans * levels * CORES * length
     chunk = max(CORES * length, LANES)
     vmem = pl.BlockSpec(memory_space=pltpu.VMEM)
-    hbm = pl.BlockSpec(memory_space=pl.ANY)
+    hbm = pl.BlockSpec(memory_space=pltpu.HBM)
     slots = spans * levels
+    kept = 2 * total * heads * (2 * key_size + rotary_size)
     sems = pltpu.SemaphoreType.DMA
     keys, values = pl.pallas_call(
         functools.partial(gather_expand, spans, levels),
@@ -325,7 +364,7 @@
             jax.ShapeDtypeStruct((heads, key_size + rotary_size, total), jnp.bfloat16),
             jax.ShapeDtypeStruct((total * heads, key_size), jnp.bfloat16),
         ),
-        in_specs=[hbm, hbm, vmem, vmem, vmem],
+        in_specs=[hbm] * 5,
         out_specs=(vmem, vmem),
         scratch_shapes=[
             pltpu.VMEM(latents.shape, jnp.bfloat16),
@@ -333,12 +372,15 @@
             pltpu.VMEM((sequences, length // 2, 2 * rotary_size), jnp.bfloat16),
             pltpu.VMEM((total, latent), jnp.bfloat16),
             pltpu.VMEM((total // 2, 2 * rotary_size), jnp.bfloat16),
+            pltpu.VMEM((1, latent), jnp.float32),
+            pltpu.VMEM((latent * heads, key_size), jnp.bfloat16),
+            pltpu.VMEM((latent * heads, key_size), jnp.bfloat16),
             pltpu.VMEM((latent * heads, key_size), jnp.float32),
             pltpu.VMEM((heads * key_size, latent), jnp.bfloat16),
             pltpu.VMEM((latent, heads * key_size), jnp.bfloat16),
             pltpu.VMEM((chunk * heads, key_size), jnp.float32),
-            sems((3,)),
-            sems((spans, 2)),
+            sems((6,)),
+            sems((3, spans, 2)),
             sems((slots, 2)),
             sems((slots, 2)),
             sems((slots, 2)),

time: 36.9 us -> 36.5 us (0.989)
  Pallas kernels: 29.5 us -> 29.1 us
    pallas_call x1, Pallas kernels: 29.5 us -> 29.1 us  [shards(): pl.pallas_call(functools.partial(gather_expand, spans, levels), out_shape...]
where the time goes in v2:
time: 36.5 us; the launch traced here: 36.2 us
  Pallas kernels  29.1 us (80%)
  local copies, waits for them, and re-layouts  6.48 us (18%)
  between operations  0.65 us (2%)
    pallas_call x1, Pallas kernels, shards(): pl.pallas_call(functools.partial(gather_expand, spans, levels), out_shape...  29.1 us
    unnamed x12, local copies, waits for them, and re-layouts  6.48 us

profile of v2, /device:TPU:1, one launch (start us, length us, event | category | flops | bytes accessed | tf_op | source)
XLA Modules:
  0.0 36.2 jit_solution(16819788898625906187)
XLA Ops:
  0.6 0.0 copy-start
  0.6 0.9 %copy-done = bf16[4,64,512]{2,1,0:T(8,128)(2,1)S(1)} copy-done((bf16[4,64,512]{2,1,0:T(8,128)(2,1)S(1)}, bf16[4,64,512]{2,1,0:T(8,128)(2,1)}, u32[]{:S(2)}) %copy-start) | copy-done | bytes 262168
  1.6 0.0 copy-start.1
  1.6 0.9 %copy-done.1 = bf16[512,2,128]{2,1,0:T(2,128)(2,1)S(1)} copy-done((bf16[512,2,128]{2,1,0:T(2,128)(2,1)S(1)}, bf16[512,2,128]{2,1,0:T(2,128)(2,1)}, u32[]{:S(2)}) %copy-start.1) | copy-done | bytes 262168
  2.5 0.0 copy-start.2
  2.5 0.9 %copy-done.2 = bf16[512,2,128]{2,1,0:T(2,128)(2,1)S(1)} copy-done((bf16[512,2,128]{2,1,0:T(2,128)(2,1)S(1)}, bf16[512,2,128]{2,1,0:T(2,128)(2,1)}, u32[]{:S(2)}) %copy-start.2) | copy-done | bytes 262168
  3.5 0.0 copy-start.3
  3.5 0.8 %copy-done.3 = bf16[4,64,64]{2,1,0:T(8,128)(2,1)S(1)} copy-done((bf16[4,64,64]{2,1,0:T(8,128)(2,1)S(1)}, bf16[4,64,64]{2,1,0:T(8,128)(2,1)}, u32[]{:S(2)}) %copy-start.3) | copy-done | bytes 32792
  4.3 0.0 copy-start.4
  4.3 0.7 %copy-done.4 = f32[512]{0:T(512)S(1)} copy-done((f32[512]{0:T(512)S(1)}, f32[512]{0:T(512)}, u32[]{:S(2)}) %copy-start.4) | copy-done | bytes 2072
  5.0 29.1 %shard_map.68 = (bf16[2,192,2048]{2,1,0:T(8,128)(2,1)S(1)}, bf16[4096,128]{1,0:T(8,128)(2,1)S(1)}) custom-call(bf16[4,64,512]{2,1,0:T(8,128)(2,1)S(1)} %copy-done, bf16[4,64,64]{2,1,0:T(8,128)(2,1)S(1)} %copy-done.3, f32[1,512]{1,0:T(1,128)S(1)} %bitcast.9, bf16[1024,128]{1,0:T(8,128)(2,1)S(1)} %bitcast.7, bf16[1024,128]{1,0:T(8,128)(2,1)S(1)} %bitcast.8), custom_call_target="tpu_custom_call" | custom-call | tf_op jit(solution)/shard_map/pallas_call | solution.py:361
  34.1 1.1 %copy.9 = bf16[1,2,192,2048]{3,2,1,0:T(8,128)(2,1)} copy(bf16[1,2,192,2048]{3,2,1,0:T(8,128)(2,1)S(1)} %bitcast.5) | data formatting | bytes 3145728
  35.2 1.0 %copy.10 = bf16[1,2048,2,128]{3,2,1,0:T(2,128)(2,1)} copy(bf16[1,2048,2,128]{3,2,1,0:T(2,128)(2,1)S(1)} %bitcast.6) | data formatting | bytes 2097152
Async XLA Ops:
  0.6 1.0 %copy-start = (bf16[4,64,512]{2,1,0:T(8,128)(2,1)S(1)}, bf16[4,64,512]{2,1,0:T(8,128)(2,1)}, u32[]{:S(2)}) copy-start(bf16[4,64,512]{2,1,0:T(8,128)(2,1)} %latents.1) | copy-start | bytes 786436
  1.6 0.9 %copy-start.1 = (bf16[512,2,128]{2,1,0:T(2,128)(2,1)S(1)}, bf16[512,2,128]{2,1,0:T(2,128)(2,1)}, u32[]{:S(2)}) copy-start(bf16[512,2,128]{2,1,0:T(2,128)(2,1)} %param.8) | copy-start | bytes 786436
  2.5 0.9 %copy-start.2 = (bf16[512,2,128]{2,1,0:T(2,128)(2,1)S(1)}, bf16[512,2,128]{2,1,0:T(2,128)(2,1)}, u32[]{:S(2)}) copy-start(bf16[512,2,128]{2,1,0:T(2,128)(2,1)} %param.9) | copy-start | bytes 786436
  3.5 0.8 %copy-start.3 = (bf16[4,64,64]{2,1,0:T(8,128)(2,1)S(1)}, bf16[4,64,64]{2,1,0:T(8,128)(2,1)}, u32[]{:S(2)}) copy-start(bf16[4,64,64]{2,1,0:T(8,128)(2,1)} %rotary.1) | copy-start | bytes 98308
  4.3 0.7 %copy-start.4 = (f32[512]{0:T(512)S(1)}, f32[512]{0:T(512)}, u32[]{:S(2)}) copy-start(f32[512]{0:T(512)} %param.7) | copy-start | bytes 6148

commit v3 on v2

--- a/solution.py
+++ b/solution.py
@@ -9,7 +9,6 @@
 
 CORES = 2
 LANES = 128
-VMEM_BYTES = 67043328
 
 
 def gather_expand(
@@ -356,13 +355,12 @@
     vmem = pl.BlockSpec(memory_space=pltpu.VMEM)
     hbm = pl.BlockSpec(memory_space=pltpu.HBM)
     slots = spans * levels
-    kept = 2 * total * heads * (2 * key_size + rotary_size)
     sems = pltpu.SemaphoreType.DMA
     keys, values = pl.pallas_call(
         functools.partial(gather_expand, spans, levels),
         out_shape=(
-            jax.ShapeDtypeStruct((heads, key_size + rotary_size, total), jnp.bfloat16),
-            jax.ShapeDtypeStruct((total * heads, key_size), jnp.bfloat16),
+            pltpu.VMEM((heads, key_size + rotary_size, total), jnp.bfloat16),
+            pltpu.VMEM((total * heads, key_size), jnp.bfloat16),
         ),
         in_specs=[hbm] * 5,
         out_specs=(vmem, vmem),
@@ -391,11 +389,16 @@
             collective_id=0, has_side_effects=True, vmem_limit_bytes=40 * 1024 * 1024
         ),
     )(
-        latents,
-        rotary_rows,
-        latent_gain.reshape(1, latent),
-        key_up.reshape(latent * heads, key_size),
-        value_up.reshape(latent * heads, key_size),
+        *(
+            pltpu.with_memory_space_constraint(operand, pltpu.HBM)
+            for operand in (
+                latents,
+                rotary_rows,
+                latent_gain.reshape(1, latent),
+                key_up.reshape(latent * heads, key_size),
+                value_up.reshape(latent * heads, key_size),
+            )
+        )
     )
     return keys[None], values.reshape(1, total, heads, key_size)
 

time: 36.5 us -> 32 us (0.88)
  local copies, waits for them, and re-layouts: 6.48 us -> 2.11 us
    unnamed x12 -> x2, local copies, waits for them, and re-layouts: 6.48 us -> 2.11 us
where the time goes in v3:
time: 32 us; the launch traced here: 31.9 us
  Pallas kernels  29.1 us (91%)
  local copies, waits for them, and re-layouts  2.11 us (7%)
  between operations  0.64 us (2%)
    pallas_call x1, Pallas kernels, shards(): pl.pallas_call(functools.partial(gather_expand, spans, levels), out_shape...  29.1 us
    unnamed x2, local copies, waits for them, and re-layouts  2.11 us

profile of v3, /device:TPU:1, one launch (start us, length us, event | category | flops | bytes accessed | tf_op | source)
XLA Modules:
  0.0 31.9 jit_solution(2498524102326096087)
XLA Ops:
  0.6 29.1 %shard_map.68 = (bf16[2,192,2048]{2,1,0:T(8,128)(2,1)S(1)}, bf16[4096,128]{1,0:T(8,128)(2,1)S(1)}) custom-call(bf16[4,64,512]{2,1,0:T(8,128)(2,1)} %latents.1, bf16[4,64,64]{2,1,0:T(8,128)(2,1)} %rotary.1, f32[1,512]{1,0:T(1,128)} %bitcast.9, bf16[1024,128]{1,0:T(8,128)(2,1)} %bitcast.7, bf16[1024,128]{1,0:T(8,128)(2,1)} %bitcast.8), custom_call_target="tpu_custom_call" | custom-call | tf_op jit(solution)/shard_map/pallas_call | solution.py:359
  29.8 1.1 %copy.9 = bf16[1,2,192,2048]{3,2,1,0:T(8,128)(2,1)} copy(bf16[1,2,192,2048]{3,2,1,0:T(8,128)(2,1)S(1)} %bitcast.5) | data formatting | bytes 3145728
  30.9 1.0 %copy.10 = bf16[1,2048,2,128]{3,2,1,0:T(2,128)(2,1)} copy(bf16[1,2048,2,128]{3,2,1,0:T(2,128)(2,1)S(1)} %bitcast.6) | data formatting | bytes 2097152

commit v4 on v3

--- a/solution.py
+++ b/solution.py
@@ -344,6 +344,17 @@
 
             if step > 0:
                 cross(part, step, 0).wait_send()
+
+
+def store(keys_in, values_in, keys_out, values_out, sems):
+    copies = [
+        pltpu.make_async_copy(keys_in, keys_out, sems.at[0]),
+        pltpu.make_async_copy(values_in, values_out, sems.at[1]),
+    ]
+    for copy in copies:
+        copy.start()
+    for copy in copies:
+        copy.wait()
 
 
 def shards(spans, levels, latents, rotary_rows, latent_gain, key_up, value_up):
@@ -400,6 +411,19 @@
             )
         )
     )
+    keys, values = pl.pallas_call(
+        store,
+        out_shape=tuple(
+            jax.ShapeDtypeStruct(part.shape, part.dtype) for part in (keys, values)
+        ),
+        in_specs=[vmem, vmem],
+        out_specs=(hbm, hbm),
+        scratch_shapes=[sems((2,))],
+        compiler_params=pltpu.CompilerParams(vmem_limit_bytes=4 * 1024 * 1024),
+    )(
+        pltpu.with_memory_space_constraint(keys, pltpu.VMEM),
+        pltpu.with_memory_space_constraint(values, pltpu.VMEM),
+    )
     return keys[None], values.reshape(1, total, heads, key_size)
 
 

time: 32 us -> 31.4 us (0.981)
  local copies, waits for them, and re-layouts: 2.11 us -> 0 us
  Pallas kernels: 29.1 us -> 30.6 us
    unnamed x2 -> x0, local copies, waits for them, and re-layouts: 2.11 us -> none
    pallas_call x0 -> x1, Pallas kernels: none -> 1.51 us  [shards(): pl.pallas_call(store, out_shape=tuple((jax.ShapeDtypeStruct(part.shape, p...]
where the time goes in v4:
time: 31.4 us; the launch traced here: 31.3 us
  Pallas kernels  30.6 us (97%)
  between operations  0.64 us (2%)
    pallas_call x1, Pallas kernels, shards(): pl.pallas_call(functools.partial(gather_expand, spans, levels), out_shape...  29.1 us
    pallas_call x1, Pallas kernels, shards(): pl.pallas_call(store, out_shape=tuple((jax.ShapeDtypeStruct(part.shape, p...  1.51 us

profile of v4, /device:TPU:1, one launch (start us, length us, event | category | flops | bytes accessed | tf_op | source)
XLA Modules:
  0.0 31.3 jit_solution(3310473152532158336)
XLA Ops:
  0.6 29.1 %shard_map.68 = (bf16[2,192,2048]{2,1,0:T(8,128)(2,1)S(1)}, bf16[4096,128]{1,0:T(8,128)(2,1)S(1)}) custom-call(bf16[4,64,512]{2,1,0:T(8,128)(2,1)} %latents.1, bf16[4,64,64]{2,1,0:T(8,128)(2,1)} %rotary.1, f32[1,512]{1,0:T(1,128)} %bitcast.7, bf16[1024,128]{1,0:T(8,128)(2,1)} %bitcast.5, bf16[1024,128]{1,0:T(8,128)(2,1)} %bitcast.6), custom_call_target="tpu_custom_call" | custom-call | tf_op jit(solution)/shard_map/pallas_call | solution.py:370
  29.8 1.5 %shard_map.69 = (bf16[2,192,2048]{2,1,0:T(8,128)(2,1)}, bf16[4096,128]{1,0:T(8,128)(2,1)}) custom-call(bf16[2,192,2048]{2,1,0:T(8,128)(2,1)S(1)} %get-tuple-element.6.keys_in, bf16[4096,128]{1,0:T(8,128)(2,1)S(1)} %get-tuple-element.7.values_in), custom_call_target="tpu_custom_call" | custom-call | tf_op jit(solution)/shard_map/pallas_call | solution.py:414
